TPU v7x, 32 devices: a whole 2x2x4 slice. The times are simulated.
32 devices in a mesh: fsdp: 4 (over y, x), tenant: 4 (over z), dp: 2 (over core).
Axes of the slice: x: 2, y: 2, z: 4, core: 2. Of those that a mesh axis runs over, the one named last changes fastest.
Arguments:
- tokens: bfloat16 [3072, 5120], P(('fsdp', 'dp'), 'tenant'), may hold values from -6 to 6
- block_tenant_index: int32 [48], P(('fsdp', 'dp')), may hold values from 0 to 7
- ranks: int32 [8], replicated, may hold values from 16 to 64, as said below
- frozen_up_weight: bfloat16 [5120, 14336], P(('fsdp', 'dp'), 'tenant'), may hold values from -0.078125 to 0.078125
- tenant_down_adapters: bfloat16 [8, 64, 5120], P('tenant'), may hold values from -0.078125 to 0.078125
- tenant_up_adapters: bfloat16 [8, 64, 14336], P('tenant'), may hold values from -0.75 to 0.75
- cotangent: bfloat16 [3072, 14336], P(('fsdp', 'dp'), 'tenant'), may hold values from -6 to 6
Outputs:
- hidden_out: bfloat16 [3072, 14336], P(('fsdp', 'dp'), 'tenant')
- grad_tokens: bfloat16 [3072, 5120], P(('fsdp', 'dp'), 'tenant')
- grad_down: float32 [8, 64, 5120], P('dp', None, 'tenant')
- grad_up: float32 [8, 64, 14336], P('dp', None, 'tenant')
Inputs may be any that keep to these rules, and one draw needn't show every extreme that they name: `ranks`: multiples of 16; some tenant has rank 64.
All inputs are finite; a program needn't handle non-finite values.
Results may differ from a plain program's by a relative error of at most 0.0034.
Values may be sent and summed in bfloat16 or wider, within the bound.
A program may use at most 128 MiB of HBM per device.

v0:
```python
import jax
import jax.numpy as jnp
from jax import lax
from jax.sharding import PartitionSpec as P

BLOCK = 64
alpha_scale = 32.0
BF16 = jnp.bfloat16
F32 = jnp.float32


def nt(a, b):
    return lax.dot_general(a, b, (((1,), (1,)), ((), ())), preferred_element_type=F32)


def tn(a, b):
    return lax.dot_general(a, b, (((0,), (0,)), ((), ())), preferred_element_type=F32)


def fetch_adapter(adapter, tenant_n, dp_n):
    share = adapter.shape[1] // dp_n
    mine = lax.dynamic_slice_in_dim(adapter, lax.axis_index("dp") * share, share, axis=1)
    part = lax.all_to_all(mine, "tenant", split_axis=2, concat_axis=0, tiled=True)
    return lax.all_gather(part, "dp", axis=1, tiled=True)


def reduce_fsdp(x, fsdp_n):
    rows = x.shape[0]
    got = lax.all_to_all(
        x.astype(BF16).reshape(fsdp_n, rows // fsdp_n, x.shape[1]), "fsdp", 0, 0, tiled=True
    )
    total = jnp.sum(got.astype(F32), axis=0).astype(BF16)
    return lax.all_gather(total, "fsdp", axis=0, tiled=True).astype(F32)


def make_shards(mesh):
    tenant_n, fsdp_n, dp_n = (mesh.shape["tenant"], mesh.shape["fsdp"], mesh.shape["dp"])

    def shards(
        tokens,
        block_tenant_index,
        ranks,
        frozen_up_weight,
        tenant_down_adapters,
        tenant_up_adapters,
        cotangent,
    ):
        rows, local_d = tokens.shape
        local_f = cotangent.shape[1]
        tenants = ranks.shape[0]
        rank = tenant_down_adapters.shape[1]
        depth = frozen_up_weight.shape[0]
        blocks = fsdp_n * dp_n
        first = max(128, depth * 3 // 5 // 128 * 128) if depth > 128 else depth
        cuts = [(0, first)] + ([(first, depth)] if first < depth else [])
        weights = [
            lax.all_gather(frozen_up_weight[a:b], ("fsdp", "dp"), axis=0, tiled=True)
            for a, b in cuts
        ]
        up = fetch_adapter(tenant_up_adapters, tenant_n, dp_n).reshape(tenants * rank, local_f)
        down = fetch_adapter(tenant_down_adapters, tenant_n, dp_n).reshape(tenants * rank, local_d)
        onehot = block_tenant_index[:, None] == jnp.arange(tenants, dtype=jnp.int32)[None, :]
        sel = onehot.astype(F32)[:, None, :, None]
        own_rank = jnp.sum(jnp.where(onehot, ranks[None, :], 0), axis=1)
        keep = jnp.arange(rank, dtype=jnp.int32)[None, :] < own_rank[:, None]
        gain = jnp.where(keep, (alpha_scale / own_rank.astype(F32))[:, None], F32(0.0))

        def compact(full):
            full = full.reshape(rows // BLOCK, BLOCK, tenants, rank)
            return jnp.sum(full * sel, axis=2)

        both = jnp.concatenate([compact(nt(tokens, down)), compact(nt(cotangent, up))], axis=2)
        both = lax.psum(both, "tenant")

        def spread(values):
            scaled = (values * gain[:, None, :]).astype(BF16)
            return (scaled[:, :, None, :] * sel.astype(BF16)).reshape(rows, tenants * rank)

        adapted = spread(both[:, :, :rank])
        adapted_grad = spread(both[:, :, rank:])
        terms = jnp.concatenate([tn(adapted, cotangent), tn(adapted_grad, tokens)], axis=1)
        terms = lax.psum_scatter(terms, "dp", scatter_dimension=0, tiled=True)
        grads = reduce_fsdp(terms, fsdp_n)
        grad_up = grads[:, :local_f].reshape(tenants // dp_n, rank, local_f)
        grad_down = grads[:, local_f:].reshape(tenants // dp_n, rank, local_d)
        whole = lax.all_gather(tokens, "tenant", axis=1, tiled=True)
        whole3 = whole.reshape(rows, blocks, depth)
        hidden = jnp.dot(adapted, up, preferred_element_type=F32)
        pieces = []
        for (a, b), weight in zip(cuts, weights):
            back = nt(cotangent, weight).astype(BF16)
            n = b - a
            got = lax.all_to_all(
                back.reshape(rows, tenant_n, blocks * n // tenant_n).transpose(1, 0, 2),
                "tenant",
                0,
                0,
                tiled=True,
            )
            pieces.append(jnp.sum(got.astype(F32), axis=0).reshape(rows, blocks // tenant_n, n))
            hidden = hidden + jnp.dot(
                whole3[:, :, a:b].reshape(rows, blocks * n), weight, preferred_element_type=F32
            )
        hidden_out = hidden.astype(BF16)
        grad_base = jnp.concatenate(pieces, axis=2).reshape(rows, local_d)
        grad_tokens = (grad_base + jnp.dot(adapted_grad, down, preferred_element_type=F32)).astype(
            BF16
        )
        return (hidden_out, grad_tokens, grad_down, grad_up)

    return shards


def solution(mesh):
    return jax.shard_map(
        make_shards(mesh),
        mesh=mesh,
        in_specs=(
            P(("fsdp", "dp"), "tenant"),
            P(("fsdp", "dp")),
            P(),
            P(("fsdp", "dp"), "tenant"),
            P("tenant", None, None),
            P("tenant", None, None),
            P(("fsdp", "dp"), "tenant"),
        ),
        out_specs=(
            P(("fsdp", "dp"), "tenant"),
            P(("fsdp", "dp"), "tenant"),
            P("dp", None, "tenant"),
            P("dp", None, "tenant"),
        ),
        check_vma=False,
    )
```

profile of v0, /device:TPU:0, one launch (start us, length us, event | category | flops | bytes accessed | tf_op | source)
XLA Modules:
  0.0 595.5 jit_solution(8852192433115120866)
XLA Ops:
  7.2 1.3 constant_dynamic-slice_fusion.1
  8.5 4.0 copy.30
  12.5 4.9 reshape.171
  17.4 6.3 %all-to-all-start = ((bf16[4,2,40960]{2,1,0:T(2,128)(2,1)}), bf16[4,2,40960]{2,1,0:T(2,128)(2,1)S(1)}, u32[]{:S(2)}, u32[]{:S(2)}) async-start(bf16[4,2,40960]{2,1,0:T(2,128)(2,1)} %reshape.171), calls=%async_computation | async-start | bytes 1310720 | tf_op jit(solution)/shard_map/all_to_all | solution.py:23
  23.8 2.8 constant_dynamic-slice_fusion
  26.6 15.2 %copy.31 = bf16[2,32,14336]{1,0,2:T(2,128)(2,1)} copy(bf16[2,32,14336]{2,1,0:T(8,128)(2,1)} %constant_dynamic-slice_fusion) | data formatting | bytes 3670016
  41.9 9.4 %reshape.173 = bf16[4,2,114688]{2,1,0:T(2,128)(2,1)} reshape(bf16[14336,2,32]{2,1,0:T(2,128)(2,1)} %bitcast.65) | data formatting | bytes 3670016
  51.3 5.1 all-to-all-start.1
  56.4 2.6 reshape.172
  59.0 6.2 %copy.28 = bf16[2,32,4,1280]{3,2,1,0:T(4,128)(2,1)S(1)} copy(bf16[2,32,4,1280]{1,0,3,2:T(2,128)(2,1)} %bitcast.70) | data formatting | bytes 1310720 | tf_op jit(solution)/shard_map/all_to_all | solution.py:23
  65.2 0.9 copy.20
  66.2 32.3 %all-to-all-done.1 = bf16[4,2,114688]{2,1,0:T(2,128)(2,1)} async-done(((bf16[4,2,114688]{2,1,0:T(2,128)(2,1)}), bf16[4,2,114688]{2,1,0:T(2,128)(2,1)}, u32[]{:S(2)}, u32[]{:S(2)}) %all-to-all-start.1) | async-done | bytes 1835040 | tf_op jit(solution)/shard_map/all_to_all | solution.py:23
  98.5 6.9 %reshape.174 = bf16[14336,2,32]{2,1,0:T(2,128)(2,1)} reshape(bf16[4,2,114688]{2,1,0:T(2,128)(2,1)} %all-to-all-done.1) | data formatting | bytes 3670016
  105.4 18.1 %copy.29 = bf16[2,32,4,3584]{3,2,1,0:T(4,128)(2,1)} copy(bf16[2,32,4,3584]{1,0,3,2:T(2,128)(2,1)} %bitcast.66) | data formatting | bytes 3670016 | tf_op jit(solution)/shard_map/all_to_all | solution.py:23
  123.5 3.0 copy.24
  126.7 3.3 convolution_bitcast_fusion.1
  130.1 1.4 copy.21
  131.5 1.5 reshape.157
  132.9 5.8 all-gather.9.cloned.1.call-done
  138.7 5.0 convolution_bitcast_fusion
  143.7 1.4 copy.25
  145.1 1.5 reshape.159
  146.6 2.9 multiply_reduce_fusion.1
  149.5 0.8 pad_maximum_fusion.2
  151.4 35.2 %all-reduce.2.cloned.1.call-done = f32[6,64,128]{2,1,0:T(8,128)} async-done(((f32[6,64,128]{2,1,0:T(8,128)}), f32[6,64,128]{2,1,0:T(8,128)}) %all-reduce.2.cloned.1.call-update) | async-done | bytes 196624 | tf_op jit(solution)/shard_map/psum | solution.py:73
  186.7 1.1 fusion.3
  187.8 1.4 broadcast_multiply_fusion
  189.2 1.7 mul.91
  190.9 1.8 mul.87
  192.7 3.6 fusion.11
  196.3 5.0 fusion.10
  201.3 8.3 %pad_maximum_fusion = f32[512,4864]{1,0:T(8,128)} fusion(f32[512,1280]{1,0:T(8,128)} %fusion.11, f32[512,3584]{1,0:T(8,128)} %fusion.10), kind=kLoop, calls=%fused_computation | loop fusion | flops 2490368 | bytes 19922944 | tf_op jit(solution)/shard_map/concatenate | solution.py:81
  209.7 2.9 slice.28
  212.6 3.5 slice.26
  216.2 48.0 %all-gather.11.cloned.1.call-done = bf16[384,5120]{1,0:T(8,128)(2,1)} async-done(((bf16[384,1280]{1,0:T(8,128)(2,1)}), bf16[384,5120]{1,0:T(8,128)(2,1)}) %all-gather.11.cloned.1.call-update) | async-done | bytes 3932176 | tf_op jit(solution)/shard_map/all_gather | solution.py:86
  264.2 2.9 copy.34
  267.5 1.9 copy.35
  269.5 1.7 copy.36
  271.1 11.4 %reduce-scatter.2.cloned.1.call-done = f32[256,4864]{1,0:T(8,128)} async-done(((f32[512,4864]{1,0:T(8,128)}), f32[256,4864]{1,0:T(8,128)}) %reduce-scatter.2.cloned.1.call-update) | async-done | bytes 4980752 | tf_op jit(solution)/shard_map/reduce_scatter | solution.py:82
  282.5 4.1 convert_element_type.69
  286.6 4.6 all-to-all-start.4
  291.2 6.6 %fusion.8 = f32[384,3584]{1,0:T(8,128)} fusion(bf16[384,512]{1,0:T(8,128)(2,1)S(1)} %mul.87, bf16[512,3584]{1,0:T(8,128)(2,1)} %bitcast.82), kind=kOutput, calls=%fused_computation.33 | convolution fusion | flops 1409286144 | bytes 9568256 | tf_op jit(solution)/shard_map/dot_general | solution.py:88
  297.8 92.3 %all-gather.15.cloned.1.call-done = bf16[2048,3584]{1,0:T(8,128)(2,1)} async-done(((bf16[256,3584]{1,0:T(8,128)(2,1)}), bf16[2048,3584]{1,0:T(8,128)(2,1)}) %all-gather.15.cloned.1.call-update) | async-done | bytes 14680080 | tf_op jit(solution)/shard_map/all_gather | solution.py:57
  390.1 9.4 %convolution_convert_fusion.1 = bf16[384,2048]{1,0:T(8,128)(2,1)S(1)} fusion(bf16[384,3584]{1,0:T(8,128)(2,1)S(1)} %copy-done, bf16[2048,3584]{1,0:T(8,128)(2,1)} %all-gather.15.cloned.1.call-done), kind=kOutput, calls=%fused_computation.9 | convolution fusion | flops 5637931008 | bytes 19005440 | tf_op jit(solution)/shard_map/dot_general | solution.py:13
  399.6 1.3 copy.41
  400.9 4.6 all-to-all-start.3
  405.5 3.1 reduce_sum.62
  408.6 95.9 %all-gather.13.cloned.1.call-done = bf16[3072,3584]{1,0:T(8,128)(2,1)} async-done(((bf16[384,3584]{1,0:T(8,128)(2,1)}), bf16[3072,3584]{1,0:T(8,128)(2,1)}) %all-gather.13.cloned.1.call-update) | async-done | bytes 22020112 | tf_op jit(solution)/shard_map/all_gather | solution.py:57
  504.5 14.0 %convolution_convert_fusion = bf16[384,3072]{1,0:T(8,128)(2,1)} fusion(bf16[384,3584]{1,0:T(8,128)(2,1)S(1)} %copy-done, bf16[3072,3584]{1,0:T(8,128)(2,1)} %all-gather.13.cloned.1.call-done), kind=kOutput, calls=%fused_computation.5 | convolution fusion | flops 8456896512 | bytes 27131904 | tf_op jit(solution)/shard_map/dot_general | solution.py:13
  518.6 3.2 copy.40
  521.8 4.7 all-to-all-start.2
  526.5 11.6 %fusion.9 = f32[384,3584]{1,0:T(8,128)} fusion(bf16[384,2048]{1,0:T(8,128)(2,1)S(1)} %bitcast.87, bf16[2048,3584]{1,0:T(8,128)(2,1)} %all-gather.15.cloned.1.call-done), kind=kOutput, calls=%fused_computation.34 | convolution fusion | flops 5637144576 | bytes 21757952 | tf_op jit(solution)/shard_map/dot_general | solution.py:101
  538.1 1.7 convert_reduce_fusion.1
  539.8 1.4 reshape.166
  541.2 4.2 all-gather.17.cloned.1.call-done
  545.4 2.4 slice.36
  547.8 2.3 slice.37
  550.1 18.7 %fusion.1 = bf16[384,3584]{1,0:T(8,128)(2,1)} fusion(f32[384,3584]{1,0:T(8,128)} %fusion.9, f32[384,3584]{1,0:T(8,128)} %fusion.8, bf16[384,3072]{1,0:T(8,128)(2,1)S(1)} %bitcast.85, bf16[3072,3584]{1,0:T(8,128)(2,1)} %all-gather.13.cloned.1.call-done), kind=kOutput, calls=%fused_computation.3 | convolution fusion | flops 8459845632 | bytes 38141952 | tf_op jit(solution)/shard_map/dot_general | solution.py:101
  568.8 12.2 %all-to-all-done.2 = bf16[4,384,768]{2,1,0:T(8,128)(2,1)} async-done(((bf16[4,384,768]{2,1,0:T(8,128)(2,1)}), bf16[4,384,768]{2,1,0:T(8,128)(2,1)}, u32[]{:S(2)}, u32[]{:S(2)}) %all-to-all-start.2) | async-done | bytes 2359328 | tf_op jit(solution)/shard_map/all_to_all | solution.py:93
  581.0 2.1 convert_reduce_fusion
  583.1 0.6 reshape.164
  583.8 2.0 pad_maximum_fusion.1
  585.9 1.2 copy-done.5
  587.1 1.6 fusion.2
  (42 shorter events, 2.1 us)
Async XLA Ops:
  7.2 131.6 %copy-start = (bf16[384,3584]{1,0:T(8,128)(2,1)S(1)}, bf16[384,3584]{1,0:T(8,128)(2,1)}, u32[]{:S(2)}) copy-start(bf16[384,3584]{1,0:T(8,128)(2,1)} %param.13) | copy-start | bytes 8257540
  17.4 33.8 %all-to-all-start = ((bf16[4,2,40960]{2,1,0:T(2,128)(2,1)}), bf16[4,2,40960]{2,1,0:T(2,128)(2,1)S(1)}, u32[]{:S(2)}, u32[]{:S(2)}) async-start(bf16[4,2,40960]{2,1,0:T(2,128)(2,1)} %reshape.171), calls=%async_computation | async-start | bytes 1310720 | tf_op jit(solution)/shard_map/all_to_all | solution.py:23
  51.3 47.2 %all-to-all-start.1 = ((bf16[4,2,114688]{2,1,0:T(2,128)(2,1)}), bf16[4,2,114688]{2,1,0:T(2,128)(2,1)}, u32[]{:S(2)}, u32[]{:S(2)}) async-start(bf16[4,2,114688]{2,1,0:T(2,128)(2,1)} %reshape.173), calls=%async_computation.1 | async-start | bytes 3670016 | tf_op jit(solution)/shard_map/all_to_all | solution.py:23
  56.4 70.4 %all-gather.7.cloned.1.call-start = ((), (), s32[]{:S(2)}) async-start(), calls=%async_computation.6 | async-start | bytes 1966080 | tf_op jit(solution)/shard_map/all_gather | solution.py:24
  66.1 72.6 %all-gather.9.cloned.1.call-start = ((), (), s32[]{:S(2)}) async-start(), calls=%async_computation.7 | async-start | bytes 5505024 | tf_op jit(solution)/shard_map/all_gather | solution.py:24
  123.5 3.1 copy-start.6
  126.6 60.1 %all-reduce.2.cloned.1.call-start = ((), (), s32[]{:S(2)}) async-start(), calls=%async_computation.8 | async-start | bytes 393216 | tf_op jit(solution)/shard_map/psum | solution.py:73
  146.6 4.6 copy-start.7
  150.3 113.9 %all-gather.11.cloned.1.call-start = ((), (), s32[]{:S(2)}) async-start(), calls=%async_computation.9 | async-start | bytes 4915200 | tf_op jit(solution)/shard_map/all_gather | solution.py:86
  150.9 131.6 %reduce-scatter.2.cloned.1.call-start = ((), (), s32[]{:S(2)}) async-start(), calls=%async_computation.12 | async-start | bytes 14942208 | tf_op jit(solution)/shard_map/reduce_scatter | solution.py:82
  209.6 180.5 %all-gather.15.cloned.1.call-start = ((), (), s32[]{:S(2)}) async-start(), calls=%async_computation.11 | async-start | bytes 16515072 | tf_op jit(solution)/shard_map/all_gather | solution.py:57
  212.6 291.9 %all-gather.13.cloned.1.call-start = ((), (), s32[]{:S(2)}) async-start(), calls=%async_computation.10 | async-start | bytes 24772608 | tf_op jit(solution)/shard_map/all_gather | solution.py:57
  286.6 114.2 %all-to-all-start.4 = ((bf16[4,64,4864]{2,1,0:T(8,128)(2,1)}), bf16[4,64,4864]{2,1,0:T(8,128)(2,1)}, u32[]{:S(2)}, u32[]{:S(2)}) async-start(bf16[4,64,4864]{2,1,0:T(8,128)(2,1)} %bitcast.71), calls=%async_computation.5 | async-start | bytes 4980736 | tf_op jit(solution)/shard_map/all_to_all | solution.py:29
  400.9 120.9 %all-to-all-start.3 = ((bf16[4,384,512]{2,1,0:T(8,128)(2,1)}), bf16[4,384,512]{2,1,0:T(8,128)(2,1)}, u32[]{:S(2)}, u32[]{:S(2)}) async-start(bf16[4,384,512]{2,1,0:T(8,128)(2,1)} %bitcast.77), calls=%async_computation.3 | async-start | bytes 3145728 | tf_op jit(solution)/shard_map/all_to_all | solution.py:93
  405.5 139.9 %all-gather.17.cloned.1.call-start = ((), (), s32[]{:S(2)}) async-start(), calls=%async_computation.13 | async-start | bytes 3112960 | tf_op jit(solution)/shard_map/all_gather | solution.py:33
  521.8 4.7 copy-start.4
  521.8 59.2 %all-to-all-start.2 = ((bf16[4,384,768]{2,1,0:T(8,128)(2,1)}), bf16[4,384,768]{2,1,0:T(8,128)(2,1)}, u32[]{:S(2)}, u32[]{:S(2)}) async-start(bf16[4,384,768]{2,1,0:T(8,128)(2,1)} %bitcast.62), calls=%async_computation.2 | async-start | bytes 4718592 | tf_op jit(solution)/shard_map/all_to_all | solution.py:93
  545.4 2.4 copy-start.2
  547.8 2.3 copy-start.3
  585.8 1.3 copy-start.5
  585.8 2.9 copy-start.1
Sparse Core Ops, SparseCore 0:
  66.2 10.8 all-gather.6
  126.7 11.9 all-gather.8
  150.5 36.1 all-reduce.1
  188.1 76.0 all-gather.10
  266.4 16.1 reduce-scatter.1
  284.3 105.8 all-gather.14
  392.6 111.8 all-gather.12
  506.9 38.4 all-gather.16
where the time goes:
time: 598 us; the launch traced here: 596 us
  waiting for transfers between devices  338 us (57%)
  local copies, waits for them, and re-layouts  111 us (19%)
  matrix products  79 us (13%)
  other arithmetic  27.8 us (5%)
  starting transfers between devices  25.8 us (4%)
  between operations  14.3 us (2%)
    all_gather x2, waiting for transfers between devices, shards(): lax.all_gather(frozen_up_weight[a:b], ('fsdp', 'dp'), axis=0, tiled=True)  188 us
    unnamed x26, local copies, waits for them, and re-layouts  51 us
    all_gather x1, waiting for transfers between devices, shards(): whole = lax.all_gather(tokens, 'tenant', axis=1, tiled=True)  48 us
    psum x1, waiting for transfers between devices, shards(): both = lax.psum(both, 'tenant')  35.2 us
    all_to_all x2, waiting for transfers between devices, fetch_adapter(): lax.all_to_all(mine, 'tenant', split_axis=2, concat_axis=0, tiled=True)  32.3 us
    dot_general x4, matrix products, nt(): lax.dot_general(a, b, (((1,), (1,)), ((), ())), preferred_element_type=F32)  31.8 us
    dot_general x2, matrix products, shards(): jnp.dot(whole3[:, :, a:b].reshape(rows, blocks * n), weight, preferred_el...  30.3 us
    all_to_all x4, local copies, waits for them, and re-layouts, fetch_adapter(): lax.all_to_all(mine, 'tenant', split_axis=2, concat_axis=0, tiled=True)  28.3 us
  transfers between devices with their start and end apart: 13, of which 9 were waited for; matrix products, arithmetic and copies ran while one was open for 32% of the time, Pallas kernels for 0%

commit v1 on v0

--- a/solution.py
+++ b/solution.py
@@ -1,3 +1,4 @@
+import functools
 import jax
 import jax.numpy as jnp
 from jax import lax
@@ -7,6 +8,17 @@
 alpha_scale = 32.0
 BF16 = jnp.bfloat16
 F32 = jnp.float32
+
+
+def enter_pairs_all(view, dimension_no, axis_no):
+    front = lax.axis_size("tenant")
+    parts_out = jnp.split(view, front, dimension_no)
+    w1 = jnp.stack(parts_out, axis=0)
+    y2 = lax.all_to_all(w1, "tenant", 0, 0)
+    return jnp.concatenate(y2, axis_no)
+
+
+open_the_case = functools.partial(enter_pairs_all, dimension_no=2, axis_no=0)
 
 
 def nt(a, b):
@@ -20,7 +32,7 @@
 def fetch_adapter(adapter, tenant_n, dp_n):
     share = adapter.shape[1] // dp_n
     mine = lax.dynamic_slice_in_dim(adapter, lax.axis_index("dp") * share, share, axis=1)
-    part = lax.all_to_all(mine, "tenant", split_axis=2, concat_axis=0, tiled=True)
+    part = open_the_case(mine)
     return lax.all_gather(part, "dp", axis=1, tiled=True)
 
 

time: 598 us -> 550 us (0.920)
  local copies, waits for them, and re-layouts: 111 us -> 38 us
  waiting for transfers between devices: 338 us -> 362 us
    unnamed x26 -> x22, local copies, waits for them, and re-layouts: 51 us -> 7.95 us
    all_to_all x4 -> x0, local copies, waits for them, and re-layouts: 28.3 us -> none  [fetch_adapter(): lax.all_to_all(mine, 'tenant', split_axis=2, concat_axis=0, tiled=True)]
    all_to_all x2, waiting for transfers between devices: 32.3 us -> 55.7 us  [enter_pairs_all(): y2 = lax.all_to_all(w1, 'tenant', 0, 0)]
  transfers between devices with their start and end apart: 13 -> 13, of which waited for: 9 -> 10; matrix products, arithmetic and copies ran while one was open for 32% -> 23% of each run, Pallas kernels for 0% -> 0%
where the time goes in v1:
time: 550 us; the launch traced here: 549 us
  waiting for transfers between devices  362 us (66%)
  matrix products  79 us (14%)
  local copies, waits for them, and re-layouts  38 us (7%)
  other arithmetic  30.2 us (5%)
  starting transfers between devices  25.2 us (5%)
  between operations  14.3 us (3%)
    all_gather x2, waiting for transfers between devices, shards(): lax.all_gather(frozen_up_weight[a:b], ('fsdp', 'dp'), axis=0, tiled=True)  188 us
    all_to_all x2, waiting for transfers between devices, enter_pairs_all(): y2 = lax.all_to_all(w1, 'tenant', 0, 0)  55.7 us
    all_gather x1, waiting for transfers between devices, shards(): whole = lax.all_gather(tokens, 'tenant', axis=1, tiled=True)  47.8 us
    psum x1, waiting for transfers between devices, shards(): both = lax.psum(both, 'tenant')  35.4 us
    dot_general x4, matrix products, nt(): lax.dot_general(a, b, (((1,), (1,)), ((), ())), preferred_element_type=F32)  31.8 us
    dot_general x2, matrix products, shards(): jnp.dot(whole3[:, :, a:b].reshape(rows, blocks * n), weight, preferred_el...  30.3 us
    all_to_all x2, waiting for transfers between devices, shards(): lax.all_to_all(back.reshape(rows, tenant_n, blocks * n // tenant_n).trans...  12.2 us
    reduce_scatter x1, waiting for transfers between devices, shards(): terms = lax.psum_scatter(terms, 'dp', scatter_dimension=0, tiled=True)  11.4 us
  transfers between devices with their start and end apart: 13, of which 10 were waited for; matrix products, arithmetic and copies ran while one was open for 23% of the time, Pallas kernels for 0%

profile of v1, /device:TPU:0, one launch (start us, length us, event | category | flops | bytes accessed | tf_op | source)
XLA Modules:
  0.0 548.7 jit_solution(15787968671821705637)
XLA Ops:
  7.2 1.4 dynamic-slice_bitcast_fusion.7
  8.5 0.9 pad_maximum_fusion.3
  9.5 6.3 %all-to-all-start = ((bf16[4,2,32,1280]{3,2,1,0:T(8,128)(2,1)}), bf16[4,2,32,1280]{3,2,1,0:T(8,128)(2,1)S(1)}, u32[]{:S(2)}, u32[]{:S(2)}) async-start(bf16[4,2,32,1280]{3,2,1,0:T(8,128)(2,1)} %pad_maximum_fusion.3), calls=%async_computation | async-start | bytes 1310720 | tf_op jit(solution)/shard_map/all_to_all | solution.py:17
  15.8 1.6 dynamic-slice_bitcast_fusion.3
  17.4 1.5 pad_maximum_fusion.2
  18.9 14.2 %all-to-all-done = bf16[4,2,32,1280]{3,2,1,0:T(8,128)(2,1)S(1)} async-done(((bf16[4,2,32,1280]{3,2,1,0:T(8,128)(2,1)}), bf16[4,2,32,1280]{3,2,1,0:T(8,128)(2,1)S(1)}, u32[]{:S(2)}, u32[]{:S(2)}) %all-to-all-start) | async-done | bytes 655392 | tf_op jit(solution)/shard_map/all_to_all | solution.py:17
  33.1 4.4 all-to-all-start.1
  37.6 0.7 all-gather.7.cloned.1.call-update
  38.3 41.4 %all-to-all-done.1 = bf16[4,2,32,3584]{3,2,1,0:T(8,128)(2,1)} async-done(((bf16[4,2,32,3584]{3,2,1,0:T(8,128)(2,1)}), bf16[4,2,32,3584]{3,2,1,0:T(8,128)(2,1)}, u32[]{:S(2)}, u32[]{:S(2)}) %all-to-all-start.1) | async-done | bytes 1835040 | tf_op jit(solution)/shard_map/all_to_all | solution.py:17
  79.9 3.3 convolution_bitcast_fusion.1
  83.2 1.4 copy.14
  84.6 1.5 reshape.164
  86.1 5.8 %all-gather.9.cloned.1.call-done = bf16[8,64,3584]{2,1,0:T(8,128)(2,1)} async-done(((bf16[8,32,3584]{2,1,0:T(8,128)(2,1)}), bf16[8,64,3584]{2,1,0:T(8,128)(2,1)}) %all-gather.9.cloned.1.call-update) | async-done | bytes 3670032 | tf_op jit(solution)/shard_map/all_gather | solution.py:36
  91.9 5.0 convolution_bitcast_fusion
  96.9 1.4 copy.15
  98.3 1.5 reshape.167
  99.8 2.9 multiply_reduce_fusion.1
  102.7 0.8 pad_maximum_fusion.4
  103.6 0.5 all-gather.11.cloned.1.call-update
  104.2 0.2 select_reduce_fusion
  104.4 35.4 %all-reduce.2.cloned.1.call-done = f32[6,64,128]{2,1,0:T(8,128)} async-done(((f32[6,64,128]{2,1,0:T(8,128)}), f32[6,64,128]{2,1,0:T(8,128)}) %all-reduce.2.cloned.1.call-update) | async-done | bytes 196624 | tf_op jit(solution)/shard_map/psum | solution.py:85
  139.8 1.1 fusion.3
  141.0 1.4 broadcast_multiply_fusion
  142.3 1.7 mul.91
  144.1 1.8 mul.87
  145.9 3.6 fusion.11
  149.4 5.0 fusion.10
  154.5 8.3 %pad_maximum_fusion = f32[512,4864]{1,0:T(8,128)} fusion(f32[512,1280]{1,0:T(8,128)} %fusion.11, f32[512,3584]{1,0:T(8,128)} %fusion.10), kind=kLoop, calls=%fused_computation | loop fusion | flops 2490368 | bytes 19922944 | tf_op jit(solution)/shard_map/concatenate | solution.py:93
  162.8 2.9 slice.28
  165.8 0.2 all-gather.13.cloned.1.call-start
  166.0 3.5 slice.26
  169.5 47.8 %all-gather.11.cloned.1.call-done = bf16[384,5120]{1,0:T(8,128)(2,1)} async-done(((bf16[384,1280]{1,0:T(8,128)(2,1)}), bf16[384,5120]{1,0:T(8,128)(2,1)}) %all-gather.11.cloned.1.call-update) | async-done | bytes 3932176 | tf_op jit(solution)/shard_map/all_gather | solution.py:98
  217.4 2.9 copy.20
  220.3 0.1 slice.34
  220.4 0.2 slice.33
  220.7 2.0 copy.21
  222.6 1.7 copy.22
  224.3 11.4 %reduce-scatter.2.cloned.1.call-done = f32[256,4864]{1,0:T(8,128)} async-done(((f32[512,4864]{1,0:T(8,128)}), f32[256,4864]{1,0:T(8,128)}) %reduce-scatter.2.cloned.1.call-update) | async-done | bytes 4980752 | tf_op jit(solution)/shard_map/reduce_scatter | solution.py:94
  235.7 4.1 convert_element_type.69
  239.8 4.5 all-to-all-start.4
  244.3 6.6 %fusion.8 = f32[384,3584]{1,0:T(8,128)} fusion(bf16[384,512]{1,0:T(8,128)(2,1)S(1)} %mul.87, bf16[512,3584]{1,0:T(8,128)(2,1)} %bitcast.84), kind=kOutput, calls=%fused_computation.41 | convolution fusion | flops 1409286144 | bytes 9568256 | tf_op jit(solution)/shard_map/dot_general | solution.py:100
  251.0 92.3 %all-gather.15.cloned.1.call-done = bf16[2048,3584]{1,0:T(8,128)(2,1)} async-done(((bf16[256,3584]{1,0:T(8,128)(2,1)}), bf16[2048,3584]{1,0:T(8,128)(2,1)}) %all-gather.15.cloned.1.call-update) | async-done | bytes 14680080 | tf_op jit(solution)/shard_map/all_gather | solution.py:69
  343.3 9.4 %convolution_convert_fusion.1 = bf16[384,2048]{1,0:T(8,128)(2,1)S(1)} fusion(bf16[384,3584]{1,0:T(8,128)(2,1)S(1)} %copy-done, bf16[2048,3584]{1,0:T(8,128)(2,1)} %all-gather.15.cloned.1.call-done), kind=kOutput, calls=%fused_computation.9 | convolution fusion | flops 5637931008 | bytes 19005440 | tf_op jit(solution)/shard_map/dot_general | solution.py:25
  352.7 1.3 copy.27
  354.0 4.6 all-to-all-start.3
  358.6 3.1 reduce_sum.62
  361.7 96.0 %all-gather.13.cloned.1.call-done = bf16[3072,3584]{1,0:T(8,128)(2,1)} async-done(((bf16[384,3584]{1,0:T(8,128)(2,1)}), bf16[3072,3584]{1,0:T(8,128)(2,1)}) %all-gather.13.cloned.1.call-update) | async-done | bytes 22020112 | tf_op jit(solution)/shard_map/all_gather | solution.py:69
  457.7 14.1 %convolution_convert_fusion = bf16[384,3072]{1,0:T(8,128)(2,1)} fusion(bf16[384,3584]{1,0:T(8,128)(2,1)S(1)} %copy-done, bf16[3072,3584]{1,0:T(8,128)(2,1)} %all-gather.13.cloned.1.call-done), kind=kOutput, calls=%fused_computation.5 | convolution fusion | flops 8456896512 | bytes 27131904 | tf_op jit(solution)/shard_map/dot_general | solution.py:25
  471.7 3.2 copy.26
  474.9 4.9 all-to-all-start.2
  479.8 11.6 %fusion.9 = f32[384,3584]{1,0:T(8,128)} fusion(bf16[384,2048]{1,0:T(8,128)(2,1)S(1)} %bitcast.88, bf16[2048,3584]{1,0:T(8,128)(2,1)} %all-gather.15.cloned.1.call-done), kind=kOutput, calls=%fused_computation.42 | convolution fusion | flops 5637144576 | bytes 21757952 | tf_op jit(solution)/shard_map/dot_general | solution.py:113
  491.4 1.7 convert_reduce_fusion.1
  493.1 1.4 reshape.174
  494.5 4.0 all-gather.17.cloned.1.call-done
  498.5 2.4 slice.36
  500.9 2.3 slice.37
  503.2 18.7 %fusion.1 = bf16[384,3584]{1,0:T(8,128)(2,1)} fusion(f32[384,3584]{1,0:T(8,128)} %fusion.9, f32[384,3584]{1,0:T(8,128)} %fusion.8, bf16[384,3072]{1,0:T(8,128)(2,1)S(1)} %bitcast.86, bf16[3072,3584]{1,0:T(8,128)(2,1)} %all-gather.13.cloned.1.call-done), kind=kOutput, calls=%fused_computation.3 | convolution fusion | flops 8459845632 | bytes 38141952 | tf_op jit(solution)/shard_map/dot_general | solution.py:113
  522.0 12.2 %all-to-all-done.2 = bf16[4,384,768]{2,1,0:T(8,128)(2,1)} async-done(((bf16[4,384,768]{2,1,0:T(8,128)(2,1)}), bf16[4,384,768]{2,1,0:T(8,128)(2,1)}, u32[]{:S(2)}, u32[]{:S(2)}) %all-to-all-start.2) | async-done | bytes 2359328 | tf_op jit(solution)/shard_map/all_to_all | solution.py:105
  534.2 2.1 convert_reduce_fusion
  536.3 0.6 reshape.172
  536.9 2.0 pad_maximum_fusion.1
  538.9 0.1 copy.23
  539.1 1.2 copy-done.6
  540.2 1.6 fusion.2
  (36 shorter events, 0.6 us)
Async XLA Ops:
  7.2 84.7 %copy-start = (bf16[384,3584]{1,0:T(8,128)(2,1)S(1)}, bf16[384,3584]{1,0:T(8,128)(2,1)}, u32[]{:S(2)}) copy-start(bf16[384,3584]{1,0:T(8,128)(2,1)} %param.13) | copy-start | bytes 8257540
  9.5 23.6 %all-to-all-start = ((bf16[4,2,32,1280]{3,2,1,0:T(8,128)(2,1)}), bf16[4,2,32,1280]{3,2,1,0:T(8,128)(2,1)S(1)}, u32[]{:S(2)}, u32[]{:S(2)}) async-start(bf16[4,2,32,1280]{3,2,1,0:T(8,128)(2,1)} %pad_maximum_fusion.3), calls=%async_computation | async-start | bytes 1310720 | tf_op jit(solution)/shard_map/all_to_all | solution.py:17
  18.9 60.9 %copy-start.7 = (s32[6]{0:T(128)S(1)}, s32[6]{0:T(128)}, u32[]{:S(2)}) copy-start(s32[6]{0:T(128)} %param.8) | copy-start | bytes 76
  33.1 4.5 copy-start.3
  33.1 46.6 %all-to-all-start.1 = ((bf16[4,2,32,3584]{3,2,1,0:T(8,128)(2,1)}), bf16[4,2,32,3584]{3,2,1,0:T(8,128)(2,1)}, u32[]{:S(2)}, u32[]{:S(2)}) async-start(bf16[4,2,32,3584]{3,2,1,0:T(8,128)(2,1)} %pad_maximum_fusion.2), calls=%async_computation.1 | async-start | bytes 3670016 | tf_op jit(solution)/shard_map/all_to_all | solution.py:17
  37.5 42.4 %all-gather.7.cloned.1.call-start = ((), (), s32[]{:S(2)}) async-start(), calls=%async_computation.6 | async-start | bytes 1966080 | tf_op jit(solution)/shard_map/all_gather | solution.py:36
  38.3 53.6 %all-gather.9.cloned.1.call-start = ((), (), s32[]{:S(2)}) async-start(), calls=%async_computation.7 | async-start | bytes 5505024 | tf_op jit(solution)/shard_map/all_gather | solution.py:36
  79.8 60.1 %all-reduce.2.cloned.1.call-start = ((), (), s32[]{:S(2)}) async-start(), calls=%async_computation.8 | async-start | bytes 393216 | tf_op jit(solution)/shard_map/psum | solution.py:85
  99.8 4.4 copy-start.8
  103.5 113.9 %all-gather.11.cloned.1.call-start = ((), (), s32[]{:S(2)}) async-start(), calls=%async_computation.9 | async-start | bytes 4915200 | tf_op jit(solution)/shard_map/all_gather | solution.py:98
  104.1 131.6 %reduce-scatter.2.cloned.1.call-start = ((), (), s32[]{:S(2)}) async-start(), calls=%async_computation.12 | async-start | bytes 14942208 | tf_op jit(solution)/shard_map/reduce_scatter | solution.py:94
  162.8 180.5 %all-gather.15.cloned.1.call-start = ((), (), s32[]{:S(2)}) async-start(), calls=%async_computation.11 | async-start | bytes 16515072 | tf_op jit(solution)/shard_map/all_gather | solution.py:69
  165.8 291.9 %all-gather.13.cloned.1.call-start = ((), (), s32[]{:S(2)}) async-start(), calls=%async_computation.10 | async-start | bytes 24772608 | tf_op jit(solution)/shard_map/all_gather | solution.py:69
  239.8 114.2 %all-to-all-start.4 = ((bf16[4,64,4864]{2,1,0:T(8,128)(2,1)}), bf16[4,64,4864]{2,1,0:T(8,128)(2,1)}, u32[]{:S(2)}, u32[]{:S(2)}) async-start(bf16[4,64,4864]{2,1,0:T(8,128)(2,1)} %bitcast.75), calls=%async_computation.5 | async-start | bytes 4980736 | tf_op jit(solution)/shard_map/all_to_all | solution.py:41
  354.0 120.9 %all-to-all-start.3 = ((bf16[4,384,512]{2,1,0:T(8,128)(2,1)}), bf16[4,384,512]{2,1,0:T(8,128)(2,1)}, u32[]{:S(2)}, u32[]{:S(2)}) async-start(bf16[4,384,512]{2,1,0:T(8,128)(2,1)} %bitcast.79), calls=%async_computation.3 | async-start | bytes 3145728 | tf_op jit(solution)/shard_map/all_to_all | solution.py:105
  358.6 139.9 %all-gather.17.cloned.1.call-start = ((), (), s32[]{:S(2)}) async-start(), calls=%async_computation.13 | async-start | bytes 3112960 | tf_op jit(solution)/shard_map/all_gather | solution.py:45
  474.9 4.9 copy-start.5
  474.9 59.3 %all-to-all-start.2 = ((bf16[4,384,768]{2,1,0:T(8,128)(2,1)}), bf16[4,384,768]{2,1,0:T(8,128)(2,1)}, u32[]{:S(2)}, u32[]{:S(2)}) async-start(bf16[4,384,768]{2,1,0:T(8,128)(2,1)} %bitcast.70), calls=%async_computation.2 | async-start | bytes 4718592 | tf_op jit(solution)/shard_map/all_to_all | solution.py:105
  498.5 2.4 copy-start.2
  500.9 2.3 copy-start.4
  538.9 1.3 copy-start.6
  538.9 2.9 copy-start.1
Sparse Core Ops, SparseCore 0:
  40.5 10.8 all-gather.6
  79.9 11.9 all-gather.8
  103.6 36.1 all-reduce.1
  141.3 76.0 all-gather.10
  219.5 16.1 reduce-scatter.1
  237.4 105.7 all-gather.14
  345.7 111.8 all-gather.12
  460.1 38.4 all-gather.16
